TPU v7x, 32 devices: a whole 2x2x4 slice. The times are simulated.
32 devices in a mesh: gz: 2 (over z_hi), gy: 4 (over z_lo, core), gx: 4 (over y, x).
Axes of the slice: x: 2, y: 2, z: 4 (z_hi: 2, z_lo: 2; z = z_hi * 2 + z_lo), core: 2. Of those that a mesh axis runs over, the one named last changes fastest.
Arguments:
- charges: float32 [65536], P(('gz', 'gy', 'gx')), may hold values from -2.5 to 2.5
- fractions: float32 [3, 65536], P(None, ('gz', 'gy', 'gx')), may hold values from 0 to 1
- base_cells: int32 [3, 65536], P(None, ('gz', 'gy', 'gx')), may hold values from 0 to 255, as said below
- counts: int32 [2, 4, 4], P('gz', 'gy', 'gx'), may hold values from 1024 to 2048, as said below
Outputs:
- forces: float32 [3, 65536], P(None, ('gz', 'gy', 'gx'))
Inputs may be any that keep to these rules, and one draw needn't show every extreme that they name: `base_cells`: atom slots of the block at gz, gy, gx have base cells inside that block's cells: x in gx*64 to gx*64 + 63, y in gy*64 to gy*64 + 63, z in gz*128 to gz*128 + 127. The first counts[b] slots of block b hold atoms, the rest are empty; some block is full in every draw.
All inputs are finite; a program needn't handle non-finite values.
Results may differ from a plain program's by a relative error of at most 0.0003.
Values sent between devices are 32-bit elements; how exact they have to be, the bound alone decides.
A program may use at most 256 MiB of HBM per device.

v0:
```python
import jax
import jax.numpy as jnp
from jax import lax
from jax.sharding import PartitionSpec as P

GRID = 256
ORDER = 4


coulomb = 332.0636
ewald = 0.7
highest = lax.Precision.HIGHEST


def from_behind(value, axis, steps):
    count = lax.axis_size(axis)
    pairs = [(source, (source + steps) % count) for source in range(count)]
    return lax.ppermute(value, axis, pairs)


def spline_weights(frac):
    rest = 1.0 - frac
    square = frac * frac
    cube = square * frac
    weights = jnp.stack(
        [
            rest * rest * rest / 6.0,
            (3.0 * cube - 6.0 * square + 4.0) / 6.0,
            (-3.0 * cube + 3.0 * square + 3.0 * frac + 1.0) / 6.0,
            cube / 6.0,
        ]
    )
    slopes = jnp.stack(
        [-0.5 * rest * rest, 1.5 * square - 2.0 * frac, -1.5 * square + frac + 0.5, 0.5 * square]
    )
    return (weights, slopes)


def green_factors(index, length):
    signed = jnp.where(2 * index < length, index, index - length).astype(jnp.float32)
    bspline = 36.0 / (4.0 + 2.0 * jnp.cos(index.astype(jnp.float32) * (2.0 * jnp.pi / length))) ** 2
    bspline = jnp.where(2 * index == length, 0.0, bspline)
    return (signed * signed, bspline)


def place_rows(values, lowest, length):
    offset = jnp.arange(length, dtype=jnp.int32)[:, None] - lowest[None, :]
    placed = jnp.zeros((length, lowest.shape[0]), jnp.float32)
    for order_index in range(values.shape[0]):
        placed = placed + jnp.where(offset == order_index, values[order_index][None, :], 0.0)
    return placed


def turn_table(first, second, length):
    product = first[:, None] * second[None, :] % length
    angle = product.astype(jnp.float32) * (2.0 * jnp.pi / length)
    return (jnp.cos(angle), jnp.sin(angle))


def window_cells(pieces, block, span, length):
    window = jnp.arange(pieces * span, dtype=jnp.int32)
    return (window // span * block + window % span) % length


def fold_rims(data, pieces, block, span, ghost_width):
    shape = data.shape
    parts = data.reshape(shape[:-1] + (pieces, span))
    carried = jnp.roll(parts[..., block:], 1, axis=len(shape) - 1)
    parts = jnp.concatenate(
        [parts[..., :ghost_width] + carried, parts[..., ghost_width:block]], axis=len(shape)
    )
    return parts.reshape(shape[:-1] + (pieces * block,))


def y_shift(data, by):
    return from_behind(data, "gy", by)


def slab_exchange(data):
    return lax.all_to_all(data, "gz", split_axis=1, concat_axis=2, tiled=True)


def column_exchange(data):
    return (
        lax.all_to_all(data[0], "gx", split_axis=1, concat_axis=2, tiled=True),
        lax.all_to_all(data[1], "gx", split_axis=1, concat_axis=2, tiled=True),
    )


def row_exchange(data):
    moved = (
        lax.all_to_all(data[0], ("gz", "gy"), split_axis=1, concat_axis=2, tiled=True),
        lax.all_to_all(data[1], ("gz", "gy"), split_axis=1, concat_axis=2, tiled=True),
    )
    return moved


def per_device(charges, fractions, base_cells, counts):

    def x_shift(data, by):
        return from_behind(data, "gx", by)

    count_x = lax.axis_size("gx")
    count_y = lax.axis_size("gy")
    count_z = lax.axis_size("gz")
    index_x = lax.axis_index("gx")
    index_y = lax.axis_index("gy")
    index_z = lax.axis_index("gz")
    cells_x = GRID // count_x
    cells_y = GRID // count_y
    cells_z = GRID // count_z
    ghost_width = ORDER - 1
    span_x = cells_x + ghost_width
    span_y = cells_y + ghost_width
    span_z = cells_z + ghost_width
    width_b = cells_y // count_z
    kept = GRID // 2
    width_k = kept // count_x
    width_u = GRID // (count_z * count_y)
    capacity = charges.shape[0]
    live = jnp.arange(capacity, dtype=jnp.int32) < counts.reshape(())
    charge = jnp.where(live, charges, jnp.zeros_like(charges))
    weights_x, slopes_x = spline_weights(fractions[0])
    weights_y, slopes_y = spline_weights(fractions[1])
    weights_z, slopes_z = spline_weights(fractions[2])
    lowest_x = base_cells[0] - index_x * cells_x
    lowest_y = base_cells[1] - index_y * cells_y
    lowest_z = base_cells[2] - index_z * cells_z
    rows_x = place_rows(weights_x, lowest_x, span_x)
    grads_x = place_rows(slopes_x, lowest_x, span_x)
    rows_y = place_rows(weights_y, lowest_y, span_y)
    grads_y = place_rows(slopes_y, lowest_y, span_y)
    rows_z = place_rows(weights_z, lowest_z, span_z)
    grads_z = place_rows(slopes_z, lowest_z, span_z)
    pairs = (rows_x[:, None, :] * rows_y[None, :, :]).reshape(span_x * span_y, capacity)
    weighted_z = rows_z * charge[None, :]
    grid = lax.dot_general(
        pairs,
        weighted_z,
        (((1,), (1,)), ((), ())),
        precision=highest,
        preferred_element_type=jnp.float32,
    ).reshape(span_x, span_y, span_z)
    arrived = x_shift(grid[cells_x:], 1)
    grid = jnp.concatenate([grid[:ghost_width] + arrived, grid[ghost_width:cells_x]], axis=0)
    arrived = y_shift(grid[:, cells_y:], 1)
    grid = jnp.concatenate([grid[:, :ghost_width] + arrived, grid[:, ghost_width:cells_y]], axis=1)
    slabs = slab_exchange(grid)
    column = fold_rims(slabs, count_z, cells_z, span_z, ghost_width)
    cell_index = jnp.arange(GRID, dtype=jnp.int32)
    freq_index = jnp.arange(kept, dtype=jnp.int32)
    cosine, sine = turn_table(cell_index, cell_index, GRID)
    cosine_front, sine_front = turn_table(cell_index, freq_index, GRID)
    real_part = jnp.einsum("xyz,zk->ykx", column, cosine_front, precision=highest)
    imag_part = -jnp.einsum("xyz,zk->ykx", column, sine_front, precision=highest)
    real_part, imag_part = column_exchange((real_part, imag_part))
    new_real = jnp.einsum("ykx,xu->kuy", real_part, cosine, precision=highest) + jnp.einsum(
        "ykx,xu->kuy", imag_part, sine, precision=highest
    )
    new_imag = jnp.einsum("ykx,xu->kuy", imag_part, cosine, precision=highest) - jnp.einsum(
        "ykx,xu->kuy", real_part, sine, precision=highest
    )
    real_part, imag_part = row_exchange((new_real, new_imag))
    source_group = cell_index // width_b
    row_in = (
        source_group % count_y * cells_y + source_group // count_y * width_b + cell_index % width_b
    )
    cosine_in, sine_in = turn_table(row_in, cell_index, GRID)
    new_real = jnp.einsum("kup,pv->kuv", real_part, cosine_in, precision=highest) + jnp.einsum(
        "kup,pv->kuv", imag_part, sine_in, precision=highest
    )
    new_imag = jnp.einsum("kup,pv->kuv", imag_part, cosine_in, precision=highest) - jnp.einsum(
        "kup,pv->kuv", real_part, sine_in, precision=highest
    )
    index_kz = index_x * width_k + jnp.arange(width_k, dtype=jnp.int32)
    index_kx = (index_z * count_y + index_y) * width_u + jnp.arange(width_u, dtype=jnp.int32)
    square_z, spline_z = green_factors(index_kz, GRID)
    square_x, spline_x = green_factors(index_kx, GRID)
    square_y, spline_y = green_factors(cell_index, GRID)
    square = square_x[None, :, None] + square_y[None, None, :] + square_z[:, None, None]
    factor = spline_x[None, :, None] * spline_y[None, None, :] * spline_z[:, None, None]
    green = jnp.where(
        square > 0.0,
        coulomb
        * jnp.exp(square * (-jnp.pi**2 / (ewald * ewald * GRID * GRID)))
        * factor
        / (jnp.pi * GRID * jnp.maximum(square, 1.0)),
        0.0,
    )
    new_real = new_real * green
    new_imag = new_imag * green
    cosine_out, sine_out = turn_table(cell_index, row_in, GRID)
    real_part = jnp.einsum("kuv,vp->kpu", new_real, cosine_out, precision=highest) - jnp.einsum(
        "kuv,vp->kpu", new_imag, sine_out, precision=highest
    )
    imag_part = jnp.einsum("kuv,vp->kpu", new_real, sine_out, precision=highest) + jnp.einsum(
        "kuv,vp->kpu", new_imag, cosine_out, precision=highest
    )
    real_part, imag_part = row_exchange((real_part, imag_part))
    cosine_x, sine_x = turn_table(cell_index, cell_index, GRID)
    new_real = jnp.einsum("kyq,qw->ywk", real_part, cosine_x, precision=highest) - jnp.einsum(
        "kyq,qw->ywk", imag_part, sine_x, precision=highest
    )
    new_imag = jnp.einsum("kyq,qw->ywk", real_part, sine_x, precision=highest) + jnp.einsum(
        "kyq,qw->ywk", imag_part, cosine_x, precision=highest
    )
    real_part, imag_part = column_exchange((new_real, new_imag))
    z_targets = window_cells(count_z, cells_z, span_z, GRID)
    cosine_z, sine_z = turn_table(freq_index, z_targets, GRID)
    doubling = jnp.where(freq_index > 0, 2.0, 1.0).astype(jnp.float32)[:, None]
    cosine_z = cosine_z * doubling
    sine_z = sine_z * doubling
    potential = jnp.einsum("yxk,kw->xwy", real_part, cosine_z, precision=highest) - jnp.einsum(
        "yxk,kw->xwy", imag_part, sine_z, precision=highest
    )
    potential = slab_exchange(potential)
    arrived = x_shift(potential[:ghost_width], -1)
    potential = jnp.concatenate([potential, arrived], axis=0)
    arrived = y_shift(potential[:, :, :ghost_width], -1)
    potential = jnp.concatenate([potential, arrived], axis=2)
    both_y = jnp.concatenate([rows_y, grads_y], axis=1)
    folded = jnp.dot(
        potential.reshape(span_x * span_z, span_y),
        both_y,
        precision=highest,
        preferred_element_type=jnp.float32,
    ).reshape(span_x, span_z, 2 * capacity)
    plain = folded[:, :, :capacity]
    sloped = folded[:, :, capacity:]
    force_x = jnp.einsum("xa,za,xza->a", grads_x, rows_z, plain, precision=highest)
    force_y = jnp.einsum("xa,za,xza->a", rows_x, rows_z, sloped, precision=highest)
    force_z = jnp.einsum("xa,za,xza->a", rows_x, grads_z, plain, precision=highest)
    return -charge[None, :] * jnp.stack([force_x, force_y, force_z])


def solution(mesh):
    in_specs = (
        P(("gz", "gy", "gx")),
        P(None, ("gz", "gy", "gx")),
        P(None, ("gz", "gy", "gx")),
        P("gz", "gy", "gx"),
    )
    out_specs = P(None, ("gz", "gy", "gx"))
    return jax.shard_map(
        per_device, mesh=mesh, in_specs=in_specs, out_specs=out_specs, check_vma=False
    )
```

profile of v0, /device:TPU:0, one launch (start us, length us, event | category | flops | bytes accessed | tf_op | source)
XLA Modules:
  0.0 918.9 jit_solution(13742035921188356109)
XLA Ops:
  6.7 13.3 %broadcast_multiply_fusion = f32[67,67,2048]{2,1,0:T(8,128)} fusion(f32[67,2048]{1,0:T(8,128)S(1)} %get-tuple-element.51, f32[67,2048]{1,0:T(8,128)S(1)} %get-tuple-element.54), kind=kLoop, calls=%fused_computation.6 | loop fusion | flops 9193472 | bytes 37871616 | tf_op jit(solution)/shard_map/mul | solution.py:135
  20.0 42.6 %mul.765 = f32[4489,2048]{1,0:T(8,128)} reshape(f32[67,67,2048]{2,1,0:T(8,128)} %broadcast_multiply_fusion) | data formatting | bytes 73547776 | tf_op jit(solution)/shard_map/mul | solution.py:135
  63.9 44.5 %fusion.22 = f32[4489,131]{0,1:T(8,128)S(1)} fusion(f32[4489,2048]{1,0:T(8,128)} %mul.765, f32[2048]{0:T(1024)S(1)} %get-tuple-element.11, f32[2048]{0:T(1024)S(1)} %bitcast.259, f32[2048]{0:T(1024)S(1)} %bitcast.261, f32[2048]{0:T(1024)S(1)} %bitcast.257, f32[2048]{0:T(1024)S(1)} %bitcast.265, s32[2048]{0:T(1024)S(1)} %bitcast.263), kind=kOutput, calls=%fused_computation.51 | convolution fusion | flops 14455625728 | bytes 39175276 | tf_op jit(solution)/shard_map/dot_general | solution.py:137
  108.7 3.5 collective-permute-start
  114.5 8.4 slice.88
  123.0 7.8 fusion.8
  130.7 4.9 copy.68
  135.6 4.9 copy.69
  140.8 5.9 copy.70
  146.7 6.8 fusion.10
  153.5 6.8 copy.71
  160.3 98.3 %all_to_all.177 = f32[64,64,131]{2,0,1:T(8,128)S(1)} all-to-all(f32[64,64,131]{2,0,1:T(8,128)} %copy.71), channel_id=1, replica_groups=mesh['gz'=2,'gy'=4,'gx'=4] {'gz'}, dimensions={1} | all-to-all | bytes 4292608 | tf_op jit(solution)/shard_map/all_to_all | solution.py:80
  286.2 4.2 reshape.493
  290.4 4.2 all-to-all-start.2
  301.1 7.9 all-to-all-done.2
  309.1 4.2 all-to-all-start.1
  313.8 4.5 reduce.13
  327.7 5.5 reduce.12
  343.9 4.4 copy.86
  348.3 5.2 reshape.497
  353.5 3.6 all-to-all-start.4
  361.1 4.4 copy.84
  365.5 4.9 reshape.495
  370.4 13.2 %all-to-all-done.4 = f32[8,1,32768]{2,1,0:T(1,128)S(1)} async-done(((f32[8,1,32768]{2,1,0:T(1,128)}), f32[8,1,32768]{2,1,0:T(1,128)S(1)}, u32[]{:S(2)}, u32[]{:S(2)}) %all-to-all-start.4) | async-done | bytes 1048608 | tf_op jit(solution)/shard_map/all_to_all | solution.py:93
  383.6 3.6 all-to-all-start.3
  393.9 5.7 copy.87
  402.9 10.7 %all-to-all-done.3 = f32[8,1,32768]{2,1,0:T(1,128)S(1)} async-done(((f32[8,1,32768]{2,1,0:T(1,128)}), f32[8,1,32768]{2,1,0:T(1,128)S(1)}, u32[]{:S(2)}, u32[]{:S(2)}) %all-to-all-start.3) | async-done | bytes 1048608 | tf_op jit(solution)/shard_map/all_to_all | solution.py:92
  420.0 5.7 copy.85
  425.7 3.5 all_to_all.142
  443.4 4.4 copy.90
  447.8 4.9 reshape.501
  452.8 3.7 all-to-all-start.6
  460.5 4.4 copy.88
  464.9 4.9 reshape.499
  469.7 13.2 %all-to-all-done.6 = f32[8,1,32768]{2,1,0:T(1,128)S(1)} async-done(((f32[8,1,32768]{2,1,0:T(1,128)}), f32[8,1,32768]{2,1,0:T(1,128)S(1)}, u32[]{:S(2)}, u32[]{:S(2)}) %all-to-all-start.6) | async-done | bytes 1048608 | tf_op jit(solution)/shard_map/all_to_all | solution.py:93
  482.9 3.6 all-to-all-start.5
  492.9 6.6 copy.157
  503.0 10.0 %all-to-all-done.5 = f32[8,1,32768]{2,1,0:T(1,128)S(1)} async-done(((f32[8,1,32768]{2,1,0:T(1,128)}), f32[8,1,32768]{2,1,0:T(1,128)S(1)}, u32[]{:S(2)}, u32[]{:S(2)}) %all-to-all-start.5) | async-done | bytes 1048608 | tf_op jit(solution)/shard_map/all_to_all | solution.py:92
  519.4 6.6 copy.158
  533.3 4.6 copy.95
  537.9 4.9 reshape.505
  542.8 4.2 all-to-all-start.8
  550.9 4.4 copy.92
  555.3 4.8 reshape.503
  560.3 4.5 all-to-all-start.7
  564.8 3.6 reduce.19
  571.8 5.3 copy.96
  577.5 3.6 reduce.18
  584.6 4.5 copy.93
  589.1 4.2 fusion.100
  593.3 4.3 subtract_bitcast_fusion
  597.6 5.4 copy.98
  603.0 4.3 reshape.507
  607.3 51.7 %all_to_all.178 = f32[2,1,268288]{2,1,0:T(1,128)} all-to-all(f32[2,1,268288]{2,1,0:T(1,128)S(1)} %reshape.507), channel_id=1, replica_groups=mesh['gz'=2,'gy'=4,'gx'=4] {'gz'}, dimensions={0} | all-to-all | bytes 4292608 | tf_op jit(solution)/shard_map/all_to_all | solution.py:80
  658.9 7.9 reduce.20
  666.9 4.3 reshape.508
  671.2 8.9 copy.149
  683.0 4.8 copy.100
  687.8 6.0 copy.103
  693.8 4.8 pad_maximum_fusion
  698.6 4.3 copy.104
  706.5 4.4 copy.105
  710.9 124.6 %fusion.2 = f32[67,131,4096]{2,1,0:T(8,128)} fusion(f32[67,131,3]{2,1,0:T(8,128)} %copy.105, f32[3,131,64]{2,1,0:T(8,128)} %copy-done.11, f32[64,131,64]{2,1,0:T(8,128)} %copy.103, f32[67,2048]{1,0:T(8,128)S(1)} %copy-done.8, f32[67,2048]{1,0:T(8,128)S(1)} %copy-done.2), kind=kOutput, calls=%fused_computation.10 | convolution fusion | flops 28905725952 | bytes 147252336 | tf_op jit(solution)/shard_map/dot_general | solution.py:222
  835.5 76.6 %multiply_reduce_fusion.1 = (f32[2048,67]{0,1:T(8,128)S(1)}, f32[2048,67]{0,1:T(8,128)S(1)}, f32[2048,67]{0,1:T(8,128)}) fusion(f32[67,131,4096]{2,1,0:T(8,128)} %fusion.2, f32[2048,131]{0,1:T(8,128)S(1)} %get-tuple-element.49, f32[2048,131]{0,1:T(8,128)S(1)} %get-tuple-element.48), kind=kLoop, calls=%fused_computation.5 | loop fusion | flops 107440128 | bytes 147595264
  (131 shorter events, 150.8 us)
Async XLA Ops:
  5.9 0.8 copy-start.1
  20.0 43.3 %copy-start.17 = (f32[2048]{0:T(1024)S(1)}, f32[2048]{0:T(1024)}, u32[]{:S(2)}) copy-start(f32[2048]{0:T(1024)} %param.4) | copy-start | bytes 24580
  108.7 14.2 %collective-permute-start = (f32[3,67,131]{1,0,2:T(4,128)S(1)}, f32[3,67,131]{1,0,2:T(4,128)S(1)}, u32[]{:S(2)}, u32[]{:S(2)}) collective-permute-start(f32[3,67,131]{1,0,2:T(4,128)S(1)} %slice.86), channel_id=1, source_target_pairs={{0,1},{1,2},{2,3},{3,0},{4,5},{5,6},{6,7},{7,4},{8,9},{9,10},{10,1... | collective-permute-start | bytes 315980 | tf_op jit(solution)/shard_map/ppermute | solution.py:18
  135.6 5.1 collective-permute-start.1
  290.4 18.7 %all-to-all-start.2 = ((f32[4,1,65536]{2,1,0:T(1,128)}), f32[4,1,65536]{2,1,0:T(1,128)}, u32[]{:S(2)}, u32[]{:S(2)}) async-start(f32[4,1,65536]{2,1,0:T(1,128)} %reshape.493), calls=%async_computation.2 | async-start | bytes 2097152 | tf_op jit(solution)/shard_map/all_to_all | solution.py:86
  309.1 18.6 %all-to-all-start.1 = ((f32[4,1,65536]{2,1,0:T(1,128)}), f32[4,1,65536]{2,1,0:T(1,128)}, u32[]{:S(2)}, u32[]{:S(2)}) async-start(f32[4,1,65536]{2,1,0:T(1,128)} %reshape.491), calls=%async_computation.1 | async-start | bytes 2097152 | tf_op jit(solution)/shard_map/all_to_all | solution.py:85
  353.5 30.1 %all-to-all-start.4 = ((f32[8,1,32768]{2,1,0:T(1,128)}), f32[8,1,32768]{2,1,0:T(1,128)S(1)}, u32[]{:S(2)}, u32[]{:S(2)}) async-start(f32[8,1,32768]{2,1,0:T(1,128)} %reshape.497), calls=%async_computation.4 | async-start | bytes 2097152 | tf_op jit(solution)/shard_map/all_to_all | solution.py:93
  383.6 30.1 %all-to-all-start.3 = ((f32[8,1,32768]{2,1,0:T(1,128)}), f32[8,1,32768]{2,1,0:T(1,128)S(1)}, u32[]{:S(2)}, u32[]{:S(2)}) async-start(f32[8,1,32768]{2,1,0:T(1,128)} %reshape.495), calls=%async_computation.3 | async-start | bytes 2097152 | tf_op jit(solution)/shard_map/all_to_all | solution.py:92
  435.7 5.4 copy-start.4
  438.0 1.0 copy-start.6
  447.8 8.7 copy-start.7
  452.8 5.7 copy-start.5
  452.8 30.2 %all-to-all-start.6 = ((f32[8,1,32768]{2,1,0:T(1,128)}), f32[8,1,32768]{2,1,0:T(1,128)S(1)}, u32[]{:S(2)}, u32[]{:S(2)}) async-start(f32[8,1,32768]{2,1,0:T(1,128)} %reshape.501), calls=%async_computation.6 | async-start | bytes 2097152 | tf_op jit(solution)/shard_map/all_to_all | solution.py:93
  482.9 30.1 %all-to-all-start.5 = ((f32[8,1,32768]{2,1,0:T(1,128)}), f32[8,1,32768]{2,1,0:T(1,128)S(1)}, u32[]{:S(2)}, u32[]{:S(2)}) async-start(f32[8,1,32768]{2,1,0:T(1,128)} %reshape.499), calls=%async_computation.5 | async-start | bytes 2097152 | tf_op jit(solution)/shard_map/all_to_all | solution.py:92
  542.8 17.5 %all-to-all-start.8 = ((f32[4,1,65536]{2,1,0:T(1,128)}), f32[4,1,65536]{2,1,0:T(1,128)S(1)}, u32[]{:S(2)}, u32[]{:S(2)}) async-start(f32[4,1,65536]{2,1,0:T(1,128)} %reshape.505), calls=%async_computation.8 | async-start | bytes 2097152 | tf_op jit(solution)/shard_map/all_to_all | solution.py:86
  560.3 17.3 %all-to-all-start.7 = ((f32[4,1,65536]{2,1,0:T(1,128)}), f32[4,1,65536]{2,1,0:T(1,128)S(1)}, u32[]{:S(2)}, u32[]{:S(2)}) async-start(f32[4,1,65536]{2,1,0:T(1,128)} %reshape.503), calls=%async_computation.7 | async-start | bytes 2097152 | tf_op jit(solution)/shard_map/all_to_all | solution.py:85
  589.1 4.2 copy-start
  681.2 12.6 %collective-permute-start.2 = (f32[3,131,64]{2,1,0:T(8,128)S(1)}, f32[3,131,64]{2,1,0:T(8,128)S(1)}, u32[]{:S(2)}, u32[]{:S(2)}) collective-permute-start(f32[3,131,64]{2,1,0:T(8,128)S(1)} %copy.102), channel_id=1, source_target_pairs={{0,3},{1,0},{2,1},{3,2},{4,7},{5,4},{6,5},{7,6},{8,11},{9,8},{10,9... | collective-permute-start | bytes 301832 | tf_op jit(solution)/shard_map/ppermute | solution.py:18
  693.8 4.8 copy-start.11
  698.6 4.3 copy-start.12
  698.6 4.3 copy-start.13
  698.6 4.3 copy-start.14
  698.6 4.3 copy-start.15
  698.6 5.0 copy-start.10
  702.9 2.2 copy-start.9
  702.9 3.6 collective-permute-start.3
  706.4 4.5 copy-start.2
  706.5 4.5 copy-start.8
  913.4 3.7 copy-start.3
  915.2 2.5 copy-start.16
where the time goes:
time: 929 us; the launch traced here: 919 us
  local copies, waits for them, and re-layouts  297 us (32%)
  matrix products  217 us (23%)
  other arithmetic  160 us (17%)
  blocking collectives  150 us (16%)
  waiting for transfers between devices  55.9 us (6%)
  starting transfers between devices  36.9 us (4%)
    all_to_all x2, blocking collectives, slab_exchange(): return lax.all_to_all(data, 'gz', split_axis=1, concat_axis=2, tiled=True)  150 us
    dot_general x1, matrix products, per_device(): jnp.dot(potential.reshape(span_x * span_z, span_y), both_y, precision=hig...  125 us
    unnamed x2, other arithmetic  77.3 us
    unnamed x59, local copies, waits for them, and re-layouts  75.9 us
    dot_general x1, matrix products, per_device(): lax.dot_general(pairs, weighted_z, (((1,), (1,)), ((), ())), precision=hi...  44.5 us
    mul x1, local copies, waits for them, and re-layouts, per_device(): rows_x[:, None, :] * rows_y[None, :, :]  42.6 us
    all_to_all x2, waiting for transfers between devices, row_exchange(): lax.all_to_all(data[1], ('gz', 'gy'), split_axis=1, concat_axis=2, tiled=...  26.4 us
    all_to_all x4, local copies, waits for them, and re-layouts, slab_exchange(): return lax.all_to_all(data, 'gz', split_axis=1, concat_axis=2, tiled=True)  22.1 us
  transfers between devices with their start and end apart: 12, of which 9 were waited for; matrix products, arithmetic and copies ran while one was open for 14% of the time, Pallas kernels for 0%

commit v1 on v0

v1 whole, which is shorter than its diff:
```python
import functools

import jax
import jax.numpy as jnp
import numpy as np
from jax import lax
from jax.experimental import pallas as pl
from jax.experimental.pallas import tpu as pltpu
from jax.sharding import PartitionSpec as P

GRID = 256
ORDER = 4


coulomb = 332.0636
ewald = 0.7
highest = lax.Precision.HIGH
gather_rows = 4


def from_behind(value, axis, steps):
    count = lax.axis_size(axis)
    pairs = [(source, (source + steps) % count) for source in range(count)]
    return lax.ppermute(value, axis, pairs)


def spline_weights(frac):
    rest = 1.0 - frac
    square = frac * frac
    cube = square * frac
    weights = jnp.stack(
        [
            rest * rest * rest / 6.0,
            (3.0 * cube - 6.0 * square + 4.0) / 6.0,
            (-3.0 * cube + 3.0 * square + 3.0 * frac + 1.0) / 6.0,
            cube / 6.0,
        ]
    )
    slopes = jnp.stack(
        [-0.5 * rest * rest, 1.5 * square - 2.0 * frac, -1.5 * square + frac + 0.5, 0.5 * square]
    )
    return (weights, slopes)


def green_factors(index, length):
    signed = jnp.where(2 * index < length, index, index - length).astype(jnp.float32)
    bspline = 36.0 / (4.0 + 2.0 * jnp.cos(index.astype(jnp.float32) * (2.0 * jnp.pi / length))) ** 2
    bspline = jnp.where(2 * index == length, 0.0, bspline)
    return (signed * signed, bspline)


def place_rows(values, lowest, length):
    offset = jnp.arange(length, dtype=jnp.int32)[:, None] - lowest[None, :]
    placed = jnp.zeros((length, lowest.shape[0]), jnp.float32)
    for order_index in range(values.shape[0]):
        placed = placed + jnp.where(offset == order_index, values[order_index][None, :], 0.0)
    return placed


def halves(value):
    high = value.astype(jnp.bfloat16)
    low = (value - high.astype(jnp.float32)).astype(jnp.bfloat16)
    return (high, low)


def rounded_halves(value):
    high = lax.reduce_precision(value, exponent_bits=8, mantissa_bits=7)
    return (high.astype(jnp.bfloat16), (value - high).astype(jnp.bfloat16))


def round_up(value, unit):
    return -(-value // unit) * unit


def spread_kernel(x_ref, y_ref, high_ref, low_ref, out_ref):
    contract = (((1,), (1,)), ((), ()))
    high, low = halves(x_ref[0] * y_ref[...])
    rows = high.shape[0]
    both = jnp.concatenate([high, low], axis=0)
    product = lax.dot_general(both, high_ref[...], contract, preferred_element_type=jnp.float32)
    rest = lax.dot_general(high, low_ref[...], contract, preferred_element_type=jnp.float32)
    out_ref[0] = product[:rows] + (product[rows:] + rest)


def spread(rows_x, rows_y, weighted_z):
    span_x, capacity = rows_x.shape
    pad_y = rows_y.shape[0]
    span_z = weighted_z.shape[0]
    high, low = rounded_halves(weighted_z)
    return pl.pallas_call(
        spread_kernel,
        grid=(span_x,),
        in_specs=[
            pl.BlockSpec((1, 1, capacity), lambda i: (i, 0, 0)),
            pl.BlockSpec((pad_y, capacity), lambda i: (0, 0)),
            pl.BlockSpec((span_z, capacity), lambda i: (0, 0)),
            pl.BlockSpec((span_z, capacity), lambda i: (0, 0)),
        ],
        out_specs=pl.BlockSpec((1, pad_y, span_z), lambda i: (i, 0, 0)),
        out_shape=jax.ShapeDtypeStruct((span_x, pad_y, span_z), jnp.float32),
    )(rows_x[:, None, :], rows_y, high, low)


def gather_kernel(width, pot_ref, z_ref, gz_ref, y_ref, gy_ref, x_ref, gx_ref, out_ref):
    block, pad_y, depth = pot_ref.shape
    capacity = out_ref.shape[1]

    @pl.when(pl.program_id(0) == 0)
    def _():
        out_ref[...] = jnp.zeros_like(out_ref)

    pot = pot_ref[...].reshape(block * pad_y, depth)

    def chunk(c, carry):
        here = pl.ds(pl.multiple_of(c * width, width), width)
        plain = jnp.dot(pot, z_ref[:, here], preferred_element_type=jnp.float32)
        sloped = jnp.dot(pot, gz_ref[:, here], preferred_element_type=jnp.float32)
        weight = y_ref[:, here]
        slope = gy_ref[:, here]
        force_x = out_ref[0:1, here]
        force_y = out_ref[1:2, here]
        force_z = out_ref[2:3, here]
        for i in range(block):
            rows = slice(i * pad_y, (i + 1) * pad_y)
            part = plain[rows]
            row_x = x_ref[i, :, here]
            force_x += gx_ref[i, :, here] * jnp.sum(weight * part, axis=0, keepdims=True)
            force_y += row_x * jnp.sum(slope * part, axis=0, keepdims=True)
            force_z += row_x * jnp.sum(weight * sloped[rows], axis=0, keepdims=True)
        out_ref[0:1, here] = force_x
        out_ref[1:2, here] = force_y
        out_ref[2:3, here] = force_z
        return carry

    lax.fori_loop(0, capacity // width, chunk, 0)


def gather(potential, rows_x, grads_x, rows_y, grads_y, rows_z, grads_z):
    span_x, span_y, span_z = potential.shape
    capacity = rows_x.shape[1]
    pad_y = rows_y.shape[0]
    pad_x = rows_x.shape[0]
    high, low = rounded_halves(potential)
    stacked = jnp.concatenate([high, low, high], axis=2)
    stacked = jnp.pad(stacked, ((0, pad_x - span_x), (0, pad_y - span_y), (0, 0)))
    high, low = rounded_halves(rows_z)
    table = jnp.concatenate([high, high, low], axis=0)
    high, low = rounded_halves(grads_z)
    slope_table = jnp.concatenate([high, high, low], axis=0)
    depth = 3 * span_z

    def whole(rows):
        return pl.BlockSpec((rows, capacity), lambda i: (0, 0))

    line = pl.BlockSpec((gather_rows, 1, capacity), lambda i: (i, 0, 0))
    return pl.pallas_call(
        functools.partial(gather_kernel, 256),
        grid=(pad_x // gather_rows,),
        in_specs=[
            pl.BlockSpec((gather_rows, pad_y, depth), lambda i: (i, 0, 0)),
            whole(depth),
            whole(depth),
            whole(pad_y),
            whole(pad_y),
            line,
            line,
        ],
        out_specs=pl.BlockSpec((3, capacity), lambda i: (0, 0)),
        out_shape=jax.ShapeDtypeStruct((3, capacity), jnp.float32),
    )(stacked, table, slope_table, rows_y, grads_y, rows_x[:, None, :], grads_x[:, None, :])


def y_shift(data, by):
    return from_behind(data, "gy", by)


def z_shift(data, by):
    return from_behind(data, "gz", by)


def exchange(data, axes):
    return lax.all_to_all(data, axes, split_axis=0, concat_axis=0, tiled=True)


def complex_turn(outputs, inputs, sign):
    angle = outputs[:, None] * inputs[None, :] % GRID * (2.0 * np.pi / GRID)
    cosine, sine = np.cos(angle), sign * np.sin(angle)
    return np.array([[cosine, -sine], [sine, cosine]])


def turn(table, data):
    return jnp.dot(
        jnp.asarray(table, jnp.float32),
        data,
        precision=highest,
        preferred_element_type=jnp.float32,
    )


def per_device(charges, fractions, base_cells, counts):

    def x_shift(data, by):
        return from_behind(data, "gx", by)

    count_x = lax.axis_size("gx")
    count_y = lax.axis_size("gy")
    count_z = lax.axis_size("gz")
    index_x = lax.axis_index("gx")
    index_y = lax.axis_index("gy")
    index_z = lax.axis_index("gz")
    cells_x = GRID // count_x
    cells_y = GRID // count_y
    cells_z = GRID // count_z
    ghost_width = ORDER - 1
    span_x = cells_x + ghost_width
    span_y = cells_y + ghost_width
    span_z = cells_z + ghost_width
    planes = count_x * count_y
    width_b = cells_x // count_y
    kept = GRID // 2
    width_k = kept // planes
    width_u = GRID // count_z
    capacity = charges.shape[0]
    live = jnp.arange(capacity, dtype=jnp.int32) < counts.reshape(())
    charge = jnp.where(live, charges, jnp.zeros_like(charges))
    weights_x, slopes_x = spline_weights(fractions[0])
    weights_y, slopes_y = spline_weights(fractions[1])
    weights_z, slopes_z = spline_weights(fractions[2])
    lowest_x = base_cells[0] - index_x * cells_x
    lowest_y = base_cells[1] - index_y * cells_y
    lowest_z = base_cells[2] - index_z * cells_z
    pad_x = round_up(span_x, gather_rows)
    pad_y = round_up(span_y, 16)
    rows_x = place_rows(weights_x, lowest_x, pad_x)
    grads_x = place_rows(slopes_x, lowest_x, pad_x)
    rows_y = place_rows(weights_y, lowest_y, pad_y)
    grads_y = place_rows(slopes_y, lowest_y, pad_y)
    rows_z = place_rows(weights_z, lowest_z, span_z)
    grads_z = place_rows(slopes_z, lowest_z, span_z)
    grid = spread(rows_x[:span_x], rows_y, rows_z * charge[None, :])[:, :span_y]
    arrived = z_shift(grid[:, :, cells_z:], 1)
    grid = jnp.concatenate(
        [grid[:, :, :ghost_width] + arrived, grid[:, :, ghost_width:cells_z]], axis=2
    )
    arrived = x_shift(grid[cells_x:], 1)
    grid = jnp.concatenate([grid[:ghost_width] + arrived, grid[ghost_width:cells_x]], axis=0)
    arrived = y_shift(grid[:, cells_y:], 1)
    grid = jnp.concatenate([grid[:, :ghost_width] + arrived, grid[:, ghost_width:cells_y]], axis=1)
    cell_index = jnp.arange(GRID, dtype=jnp.int32)
    cells = np.arange(GRID)

    data = exchange(grid.reshape(count_y, width_b, cells_y, cells_z), "gy")
    data = data.transpose(0, 2, 1, 3).reshape(GRID, width_b * cells_z)
    table = complex_turn(np.arange(kept), cells, -1.0)[:, 0]
    table = table.reshape(2, planes, width_k, GRID).transpose(1, 0, 2, 3)
    data = turn(table.reshape(2 * kept, GRID), data)
    data = exchange(data.reshape(planes, 2 * width_k, width_b * cells_z), ("gx", "gy"))
    data = data.reshape(planes, 2, width_k, width_b, cells_z).transpose(0, 1, 3, 2, 4)
    table = complex_turn(cells, cells, -1.0).reshape(2, 2, count_z, width_u, planes, width_b)
    table = table.transpose(2, 0, 3, 4, 1, 5).reshape(2 * GRID, 2 * GRID)
    data = turn(table, data.reshape(2 * GRID, width_k * cells_z))
    data = exchange(data.reshape(count_z, 2 * width_u, width_k * cells_z), "gz")
    data = data.reshape(count_z, 2, width_u, width_k, cells_z).transpose(0, 1, 4, 3, 2)
    table = complex_turn(cells, cells, -1.0).reshape(2, 2, GRID, count_z, cells_z)
    table = table.transpose(0, 2, 3, 1, 4).reshape(2 * GRID, 2 * GRID)
    data = turn(table, data.reshape(2 * GRID, width_k * width_u))
    data = data.reshape(2, GRID, width_k * width_u)
    index_ky = (index_x * count_y + index_y) * width_k + jnp.arange(width_k, dtype=jnp.int32)
    index_kx = index_z * width_u + jnp.arange(width_u, dtype=jnp.int32)
    square_y, spline_y = green_factors(index_ky, GRID)
    square_x, spline_x = green_factors(index_kx, GRID)
    square_z, spline_z = green_factors(cell_index, GRID)
    square_yx = (square_y[:, None] + square_x[None, :]).reshape(-1)
    factor_yx = (spline_y[:, None] * spline_x[None, :]).reshape(-1)
    square = square_z[:, None] + square_yx[None, :]
    factor = spline_z[:, None] * factor_yx[None, :]
    green = jnp.where(
        square > 0.0,
        coulomb
        * jnp.exp(square * (-jnp.pi**2 / (ewald * ewald * GRID * GRID)))
        * factor
        / (jnp.pi * GRID * jnp.maximum(square, 1.0)),
        0.0,
    )
    data = data * green[None]
    table = complex_turn(cells, cells, 1.0).reshape(2, 2, count_z, cells_z, GRID)
    table = table.transpose(2, 0, 3, 1, 4).reshape(2 * GRID, 2 * GRID)
    data = turn(table, data.reshape(2 * GRID, width_k * width_u))
    data = exchange(data.reshape(count_z, 2 * cells_z, width_k * width_u), "gz")
    data = data.reshape(count_z, 2, cells_z, width_k, width_u).transpose(0, 1, 4, 3, 2)
    table = complex_turn(cells, cells, 1.0).reshape(2, 2, planes, width_b, count_z, width_u)
    table = table.transpose(2, 0, 3, 4, 1, 5).reshape(2 * GRID, 2 * GRID)
    data = turn(table, data.reshape(2 * GRID, width_k * cells_z))
    data = exchange(data.reshape(planes, 2 * width_b, width_k * cells_z), ("gx", "gy"))
    data = data.reshape(planes, 2, width_b, width_k, cells_z).transpose(0, 1, 3, 2, 4)
    table = complex_turn(cells, np.arange(kept), 1.0)[0]
    table = table * np.where(np.arange(kept) > 0, 2.0, 1.0)
    table = table.reshape(2, GRID, planes, width_k).transpose(1, 2, 0, 3)
    data = turn(table.reshape(GRID, 2 * kept), data.reshape(2 * kept, width_b * cells_z))
    data = exchange(data.reshape(count_y, cells_y, width_b * cells_z), "gy")
    potential = data.reshape(count_y, cells_y, width_b, cells_z).transpose(0, 2, 1, 3)
    potential = potential.reshape(cells_x, cells_y, cells_z)
    arrived = x_shift(potential[:ghost_width], -1)
    potential = jnp.concatenate([potential, arrived], axis=0)
    arrived = y_shift(potential[:, :ghost_width], -1)
    potential = jnp.concatenate([potential, arrived], axis=1)
    arrived = z_shift(potential[:, :, :ghost_width], -1)
    potential = jnp.concatenate([potential, arrived], axis=2)
    return -charge[None, :] * gather(
        potential, rows_x, grads_x, rows_y, grads_y, rows_z, grads_z
    )


def solution(mesh):
    in_specs = (
        P(("gz", "gy", "gx")),
        P(None, ("gz", "gy", "gx")),
        P(None, ("gz", "gy", "gx")),
        P("gz", "gy", "gx"),
    )
    out_specs = P(None, ("gz", "gy", "gx"))
    return jax.shard_map(
        per_device, mesh=mesh, in_specs=in_specs, out_specs=out_specs, check_vma=False
    )
```

time: 929 us -> 420 us (0.45)
  local copies, waits for them, and re-layouts: 297 us -> 26.7 us
  matrix products: 217 us -> 13.4 us
  other arithmetic: 160 us -> 33.2 us
  Pallas kernels: 0 us -> 97.1 us
  starting transfers between devices: 36.9 us -> 10.9 us
  blocking collectives: 150 us -> 166 us
  waiting for transfers between devices: 55.9 us -> 67.1 us
    dot_general x22 -> x6, matrix products: 217 us -> 13.4 us  [turn(): jnp.dot(jnp.asarray(table, jnp.float32), data, precision=highest, preferr...]
    pallas_call x0 -> x2, Pallas kernels: none -> 97.1 us  [the longest x1 53.4 us: gather(): pl.pallas_call(functools.partial(gather_kernel, 256), grid=(pad_x // gath...]
    all_to_all x19 -> x0, local copies, waits for them, and re-layouts: 81.3 us -> none  [the longest x4 22.1 us: slab_exchange(): return lax.all_to_all(data, 'gz', split_axis=1, concat_axis=2, tiled=True)]
    unnamed x2 -> x0, other arithmetic: 77.3 us -> none
    unnamed x59 -> x20, local copies, waits for them, and re-layouts: 75.9 us -> 4.95 us
    mul x1 -> x0, local copies, waits for them, and re-layouts: 42.6 us -> none  [per_device(): rows_x[:, None, :] * rows_y[None, :, :]]
    all_to_all x9 -> x0, other arithmetic: 37.5 us -> none  [the longest x2 9.14 us: column_exchange(): lax.all_to_all(data[0], 'gx', split_axis=1, concat_axis=2, tiled=True)]
    all_to_all x8 -> x1, starting transfers between devices: 31.5 us -> 4.16 us  [exchange(): return lax.all_to_all(data, axes, split_axis=0, concat_axis=0, tiled=True)]
  transfers between devices with their start and end apart: 12 -> 7, of which waited for: 9 -> 6; matrix products, arithmetic and copies ran while one was open for 14% -> 3% of each run, Pallas kernels for 0% -> 0%
where the time goes in v1:
time: 420 us; the launch traced here: 416 us
  blocking collectives  166 us (40%)
  Pallas kernels  97.1 us (23%)
  waiting for transfers between devices  67.1 us (16%)
  other arithmetic  33.2 us (8%)
  local copies, waits for them, and re-layouts  26.7 us (6%)
  matrix products  13.4 us (3%)
  starting transfers between devices  10.9 us (3%)
    all_to_all x5, blocking collectives, exchange(): return lax.all_to_all(data, axes, split_axis=0, concat_axis=0, tiled=True)  166 us
    pallas_call x1, Pallas kernels, gather(): pl.pallas_call(functools.partial(gather_kernel, 256), grid=(pad_x // gath...  53.4 us
    all_to_all x1, waiting for transfers between devices, exchange(): return lax.all_to_all(data, axes, split_axis=0, concat_axis=0, tiled=True)  46.6 us
    pallas_call x1, Pallas kernels, spread(): pl.pallas_call(spread_kernel, grid=(span_x,), in_specs=[pl.BlockSpec((1,...  43.7 us
    ppermute x6, waiting for transfers between devices, from_behind(): return lax.ppermute(value, axis, pairs)  20.5 us
    dot_general x6, matrix products, turn(): jnp.dot(jnp.asarray(table, jnp.float32), data, precision=highest, preferr...  13.4 us
  transfers between devices with their start and end apart: 7, of which 6 were waited for; matrix products, arithmetic and copies ran while one was open for 3% of the time, Pallas kernels for 0%

profile of v1, /device:TPU:0, one launch (start us, length us, event | category | flops | bytes accessed | tf_op | source)
XLA Modules:
  0.0 415.5 jit_solution(742416021681707844)
XLA Ops:
  0.0 1.0 multiply_multiply_fusion
  1.0 0.9 multiply_multiply_fusion.1
  2.6 0.9 slice_subtract_fusion
  3.5 0.2 select_add_fusion.4
  3.7 1.2 broadcast_in_dim.265.x_ref
  4.9 1.4 select_add_fusion.2
  6.4 2.8 reduce-precision_convert_fusion.1
  9.2 43.7 %shard_map.100 = f32[67,80,131]{2,1,0:T(8,128)} custom-call(f32[67,1,2048]{2,1,0:T(1,128)} %broadcast_in_dim.265.x_ref, f32[80,2048]{1,0:T(8,128)} %get-tuple-element.47.y_ref, bf16[131,2048]{1,0:T(8,128)(2,1)} %get-tuple-element.49.high_ref, bf16[131,2048]{1,0:T(8,128)(2,1)} %get-tuple-element.48.low_ref), custom_call_target="tpu_custom_call" | custom-call | tf_op jit(solution)/shard_map/pallas_call | solution.py:90
  52.9 1.9 slice.81
  54.8 0.9 copy.17
  55.7 4.1 collective-permute-start
  59.8 2.4 slice.82
  62.3 3.0 collective-permute-done
  65.3 2.3 copy.18
  67.6 2.7 slice_add_fusion
  70.3 0.1 pad_maximum_fusion.7
  70.4 1.6 collective-permute-start.1
  72.0 4.1 collective-permute-done.1
  76.1 0.1 maximum_add_fusion
  76.2 0.7 fusion.10
  76.9 0.1 collective-permute-start.2
  77.0 0.3 slice.85
  77.3 4.1 collective-permute-done.2
  81.4 0.5 pad_maximum_fusion.3
  81.9 1.2 copy.19
  83.1 28.3 %all_to_all.30 = f32[4,16,64,128]{3,1,2,0:T(8,128)S(1)} all-to-all(f32[4,16,64,128]{3,1,2,0:T(8,128)S(1)} %copy.19), channel_id=1, replica_groups=mesh['gz'=2,'gy'=4,'gx'=4] {'gy'}, dimensions={0} | all-to-all | bytes 4194304 | tf_op jit(solution)/shard_map/all_to_all | solution.py:182
  111.4 1.6 fusion.20
  113.0 30.3 %all_to_all.31 = f32[16,16,2048]{2,1,0:T(8,128)S(1)} all-to-all(f32[16,16,2048]{2,1,0:T(8,128)S(1)} %bitcast.113), channel_id=1, replica_groups=mesh['gz'=2,'gy'=4,'gx'=4] {'gx','gy'}, dimensions={0} | all-to-all | bytes 4194304 | tf_op jit(solution)/shard_map/all_to_all | solution.py:182
  143.3 3.3 fusion.17
  146.6 4.2 %all-to-all-start.2 = ((f32[2,256,1024]{2,1,0:T(8,128)}), f32[2,256,1024]{2,1,0:T(8,128)S(1)}, u32[]{:S(2)}, u32[]{:S(2)}) async-start(f32[2,256,1024]{2,1,0:T(8,128)} %bitcast.110), calls=%async_computation.2 | async-start | bytes 4194304 | tf_op jit(solution)/shard_map/all_to_all | solution.py:182
  150.9 0.1 add_bitcast_fusion
  151.0 0.1 multiply_bitcast_fusion
  151.1 0.5 fusion.36
  151.6 46.6 %all-to-all-done.2 = f32[2,256,1024]{2,1,0:T(8,128)S(1)} async-done(((f32[2,256,1024]{2,1,0:T(8,128)}), f32[2,256,1024]{2,1,0:T(8,128)S(1)}, u32[]{:S(2)}, u32[]{:S(2)}) %all-to-all-start.2) | async-done | bytes 2097184 | tf_op jit(solution)/shard_map/all_to_all | solution.py:182
  198.2 1.8 copy.27
  200.0 2.0 copy.20
  202.1 3.4 bitcast_multiply_fusion
  205.5 1.9 fusion.62
  207.4 48.8 %all_to_all.32 = f32[2,256,1024]{2,1,0:T(8,128)S(1)} all-to-all(f32[2,256,1024]{2,1,0:T(8,128)S(1)} %bitcast.115), channel_id=1, replica_groups=mesh['gz'=2,'gy'=4,'gx'=4] {'gz'}, dimensions={0} | all-to-all | bytes 4194304 | tf_op jit(solution)/shard_map/all_to_all | solution.py:182
  256.3 1.8 copy.29
  258.1 2.1 copy.21
  260.2 2.0 fusion.11
  262.2 30.6 %all_to_all.33 = f32[16,32,1024]{2,1,0:T(8,128)S(1)} all-to-all(f32[16,32,1024]{2,1,0:T(8,128)S(1)} %bitcast.117), channel_id=1, replica_groups=mesh['gz'=2,'gy'=4,'gx'=4] {'gx','gy'}, dimensions={0} | all-to-all | bytes 4194304 | tf_op jit(solution)/shard_map/all_to_all | solution.py:182
  292.9 0.5 copy.31
  293.3 0.5 copy-done.5
  293.8 1.2 fusion.63
  295.0 28.1 %all_to_all.34 = f32[4,64,2048]{2,1,0:T(8,128)S(1)} all-to-all(f32[4,64,2048]{2,1,0:T(8,128)S(1)} %bitcast.119), channel_id=1, replica_groups=mesh['gz'=2,'gy'=4,'gx'=4] {'gy'}, dimensions={0} | all-to-all | bytes 4194304 | tf_op jit(solution)/shard_map/all_to_all | solution.py:182
  323.1 0.4 copy.32
  323.5 0.1 bitcast_bitcast_fusion
  323.7 0.6 copy.22
  324.3 0.6 collective-permute-start.3
  325.0 4.0 collective-permute-done.3
  329.0 0.1 collective-permute-start.4
  329.1 3.6 fusion.51
  332.7 1.7 pad_maximum_fusion.1
  334.4 3.3 copy.23
  337.7 0.3 collective-permute-start.5
  338.0 3.4 pad_maximum_fusion.4
  341.5 5.3 %collective-permute-done.5 = f32[67,67,3]{1,0,2:T(8,128)} collective-permute-done((f32[67,67,3]{1,0,2:T(8,128)}, f32[67,67,3]{1,0,2:T(8,128)}, u32[]{:S(2)}, u32[]{:S(2)}) %collective-permute-start.5) | collective-permute-done | bytes 53900 | tf_op jit(solution)/shard_map/ppermute | solution.py:24
  346.8 3.2 copy.24
  350.0 2.6 fusion.9
  352.6 8.2 %fusion.8.pot_ref = bf16[68,80,393]{2,1,0:T(8,128)(2,1)} fusion(bf16[67,67,131]{2,1,0:T(8,128)(2,1)S(1)} %get-tuple-element.8, bf16[67,67,131]{2,1,0:T(8,128)(2,1)S(1)} %get-tuple-element.7), kind=kLoop, calls=%fused_computation.12 | loop fusion | flops 32068800 | bytes 6628076 | tf_op jit(solution)/shard_map/concatenate | solution.py:144
  360.7 53.4 %shard_map.101 = f32[3,2048]{1,0:T(4,128)} custom-call(bf16[68,80,393]{2,1,0:T(8,128)(2,1)} %fusion.8.pot_ref, bf16[393,2048]{1,0:T(8,128)(2,1)} %get-tuple-element.54.z_ref, bf16[393,2048]{1,0:T(8,128)(2,1)} %get-tuple-element.55.gz_ref, f32[80,2048]{1,0:T(8,128)} %get-tuple-element.47.y_ref, f32[80,2048]{1,0:T(8,128)} %get-tuple-element.46.gy_ref, ...), custom_call_target="tpu_custom_call" | custom-call | tf_op jit(solution)/shard_map/pallas_call | solution.py:156
  414.1 1.4 broadcast_multiply_fusion
  (24 shorter events, 0.3 us)
Async XLA Ops:
  0.0 4.9 %copy-start.7 = (f32[2048]{0:T(1024)S(1)}, f32[2048]{0:T(1024)}, u32[]{:S(2)}) copy-start(f32[2048]{0:T(1024)} %param.10) | copy-start | bytes 24580
  55.7 9.5 %collective-permute-start = (f32[67,67,3]{1,0,2:T(8,128)S(1)}, f32[67,67,3]{1,0,2:T(8,128)S(1)}, u32[]{:S(2)}, u32[]{:S(2)}) collective-permute-start(f32[67,67,3]{1,0,2:T(8,128)S(1)} %copy.17), channel_id=1, source_target_pairs={{0,16},{16,0},{1,17},{17,1},{2,18},{18,2},{3,19},{19,3},{4,20},{20... | collective-permute-start | bytes 161612 | tf_op jit(solution)/shard_map/ppermute | solution.py:24
  70.4 5.7 %collective-permute-start.1 = (f32[3,67,128]{2,1,0:T(8,128)S(1)}, f32[3,67,128]{2,1,0:T(8,128)S(1)}, u32[]{:S(2)}, u32[]{:S(2)}) collective-permute-start(f32[3,67,128]{2,1,0:T(8,128)S(1)} %pad_maximum_fusion.7), channel_id=1, source_target_pairs={{0,1},{1,2},{2,3},{3,0},{4,5},{5,6},{6,7},{7,4},{8,9},{9,10},{10,1... | collective-permute-start | bytes 308744 | tf_op jit(solution)/shard_map/ppermute | solution.py:24
  76.9 4.4 %collective-permute-start.2 = (f32[64,3,128]{2,1,0:T(4,128)S(1)}, f32[64,3,128]{2,1,0:T(4,128)S(1)}, u32[]{:S(2)}, u32[]{:S(2)}) collective-permute-start(f32[64,3,128]{2,1,0:T(4,128)S(1)} %slice.84), channel_id=1, source_target_pairs={{0,4},{4,8},{8,12},{12,0},{1,5},{5,9},{9,13},{13,1},{2,6},{6,10},{... | collective-permute-start | bytes 294920 | tf_op jit(solution)/shard_map/ppermute | solution.py:24
  83.1 28.3 %copy-start.6 = (f32[256,256]{1,0:T(8,128)S(1)}, f32[256,256]{1,0:T(8,128)}, u32[]{:S(2)}) copy-start(f32[256,256]{1,0:T(8,128)} %constant.35.clone) | copy-start | bytes 786436
  113.0 30.3 %copy-start.4 = (f32[512,512]{1,0:T(8,128)S(1)}, f32[512,512]{1,0:T(8,128)}, u32[]{:S(2)}) copy-start(f32[512,512]{1,0:T(8,128)} %constant.36.clone) | copy-start | bytes 3145732
  146.6 51.6 %all-to-all-start.2 = ((f32[2,256,1024]{2,1,0:T(8,128)}), f32[2,256,1024]{2,1,0:T(8,128)S(1)}, u32[]{:S(2)}, u32[]{:S(2)}) async-start(f32[2,256,1024]{2,1,0:T(8,128)} %bitcast.110), calls=%async_computation.2 | async-start | bytes 4194304 | tf_op jit(solution)/shard_map/all_to_all | solution.py:182
  202.1 3.4 copy-start.3
  258.1 2.1 copy-start.2
  292.9 1.0 copy-start.5
  324.3 4.7 %collective-permute-start.3 = (f32[3,64,128]{2,1,0:T(8,128)S(1)}, f32[3,64,128]{2,1,0:T(8,128)S(1)}, u32[]{:S(2)}, u32[]{:S(2)}) collective-permute-start(f32[3,64,128]{2,1,0:T(8,128)S(1)} %slice.86), channel_id=1, source_target_pairs={{0,3},{1,0},{2,1},{3,2},{4,7},{5,4},{6,5},{7,6},{8,11},{9,8},{10,9... | collective-permute-start | bytes 294920 | tf_op jit(solution)/shard_map/ppermute | solution.py:24
  329.0 3.7 collective-permute-start.4
  334.4 3.6 copy-start
  334.4 3.6 copy-start.1
  337.7 9.0 %collective-permute-start.5 = (f32[67,67,3]{1,0,2:T(8,128)}, f32[67,67,3]{1,0,2:T(8,128)}, u32[]{:S(2)}, u32[]{:S(2)}) collective-permute-start(f32[67,67,3]{1,0,2:T(8,128)} %copy.23), channel_id=1, source_target_pairs={{0,16},{16,0},{1,17},{17,1},{2,18},{18,2},{3,19},{19,3},{4,20},{20... | collective-permute-start | bytes 161612 | tf_op jit(solution)/shard_map/ppermute | solution.py:24

commit v2 on v1

--- a/solution.py
+++ b/solution.py
@@ -74,12 +74,16 @@
 
 def spread_kernel(x_ref, y_ref, high_ref, low_ref, out_ref):
     contract = (((1,), (1,)), ((), ()))
-    high, low = halves(x_ref[0] * y_ref[...])
+    block, pad_y, span_z = out_ref.shape
+    lines = y_ref[...]
+    pairs = jnp.concatenate([x_ref[i] * lines for i in range(block)], axis=0)
+    high, low = halves(pairs)
     rows = high.shape[0]
     both = jnp.concatenate([high, low], axis=0)
     product = lax.dot_general(both, high_ref[...], contract, preferred_element_type=jnp.float32)
     rest = lax.dot_general(high, low_ref[...], contract, preferred_element_type=jnp.float32)
-    out_ref[0] = product[:rows] + (product[rows:] + rest)
+    total = product[:rows] + (product[rows:] + rest)
+    out_ref[...] = total.reshape(block, pad_y, span_z)
 
 
 def spread(rows_x, rows_y, weighted_z):
@@ -89,14 +93,14 @@
     high, low = rounded_halves(weighted_z)
     return pl.pallas_call(
         spread_kernel,
-        grid=(span_x,),
+        grid=(span_x // gather_rows,),
         in_specs=[
-            pl.BlockSpec((1, 1, capacity), lambda i: (i, 0, 0)),
+            pl.BlockSpec((gather_rows, 1, capacity), lambda i: (i, 0, 0)),
             pl.BlockSpec((pad_y, capacity), lambda i: (0, 0)),
             pl.BlockSpec((span_z, capacity), lambda i: (0, 0)),
             pl.BlockSpec((span_z, capacity), lambda i: (0, 0)),
         ],
-        out_specs=pl.BlockSpec((1, pad_y, span_z), lambda i: (i, 0, 0)),
+        out_specs=pl.BlockSpec((gather_rows, pad_y, span_z), lambda i: (i, 0, 0)),
         out_shape=jax.ShapeDtypeStruct((span_x, pad_y, span_z), jnp.float32),
     )(rows_x[:, None, :], rows_y, high, low)
 
@@ -237,7 +241,7 @@
     grads_y = place_rows(slopes_y, lowest_y, pad_y)
     rows_z = place_rows(weights_z, lowest_z, span_z)
     grads_z = place_rows(slopes_z, lowest_z, span_z)
-    grid = spread(rows_x[:span_x], rows_y, rows_z * charge[None, :])[:, :span_y]
+    grid = spread(rows_x, rows_y, rows_z * charge[None, :])[:span_x, :span_y]
     arrived = z_shift(grid[:, :, cells_z:], 1)
     grid = jnp.concatenate(
         [grid[:, :, :ghost_width] + arrived, grid[:, :, ghost_width:cells_z]], axis=2

time: 420 us -> 398 us (0.948)
  Pallas kernels: 97.1 us -> 76.3 us
    pallas_call x1, Pallas kernels: 43.7 us -> 22.9 us  [spread(): pl.pallas_call(spread_kernel, grid=(span_x // gather_rows,), in_specs=[pl...]
  transfers between devices with their start and end apart: 7 -> 7, of which waited for: 6 -> 7; matrix products, arithmetic and copies ran while one was open for 3% -> 2% of each run, Pallas kernels for 0% -> 0%
where the time goes in v2:
time: 398 us; the launch traced here: 397 us
  blocking collectives  166 us (42%)
  Pallas kernels  76.3 us (19%)
  waiting for transfers between devices  69.9 us (18%)
  other arithmetic  33.7 us (8%)
  local copies, waits for them, and re-layouts  25.5 us (6%)
  matrix products  13.4 us (3%)
  starting transfers between devices  10.8 us (3%)
    all_to_all x5, blocking collectives, exchange(): return lax.all_to_all(data, axes, split_axis=0, concat_axis=0, tiled=True)  166 us
    pallas_call x1, Pallas kernels, gather(): pl.pallas_call(functools.partial(gather_kernel, 256), grid=(pad_x // gath...  53.4 us
    all_to_all x1, waiting for transfers between devices, exchange(): return lax.all_to_all(data, axes, split_axis=0, concat_axis=0, tiled=True)  46.6 us
    ppermute x6, waiting for transfers between devices, from_behind(): return lax.ppermute(value, axis, pairs)  23.3 us
    pallas_call x1, Pallas kernels, spread(): pl.pallas_call(spread_kernel, grid=(span_x // gather_rows,), in_specs=[pl...  22.9 us
    dot_general x6, matrix products, turn(): jnp.dot(jnp.asarray(table, jnp.float32), data, precision=highest, preferr...  13.4 us
    concatenate x1, other arithmetic, gather(): stacked = jnp.concatenate([high, low, high], axis=2)  8.2 us
  transfers between devices with their start and end apart: 7, of which 7 were waited for; matrix products, arithmetic and copies ran while one was open for 2% of the time, Pallas kernels for 0%

profile of v2, /device:TPU:0, one launch (start us, length us, event | category | flops | bytes accessed | tf_op | source)
XLA Modules:
  0.0 396.8 jit_solution(926266849055088889)
XLA Ops:
  0.0 1.0 multiply_multiply_fusion
  1.0 0.9 multiply_multiply_fusion.1
  2.6 0.7 fusion.56
  3.3 0.9 slice_subtract_fusion
  4.2 3.7 fusion.47
  7.8 1.4 select_add_fusion.2
  9.3 2.9 reduce-precision_convert_fusion.1
  12.2 22.9 %shard_map.100 = f32[68,80,131]{2,1,0:T(8,128)} custom-call(f32[68,1,2048]{2,1,0:T(1,128)} %get-tuple-element.45.x_ref, f32[80,2048]{1,0:T(8,128)} %get-tuple-element.47.y_ref, bf16[131,2048]{1,0:T(8,128)(2,1)} %get-tuple-element.49.high_ref, bf16[131,2048]{1,0:T(8,128)(2,1)} %get-tuple-element.48.low_ref), custom_call_target="tpu_custom_call" | custom-call | tf_op jit(solution)/shard_map/pallas_call | solution.py:94
  35.1 1.9 slice.77
  37.0 0.9 copy.17
  37.9 4.1 %collective-permute-start = (f32[67,67,3]{1,0,2:T(8,128)S(1)}, f32[67,67,3]{1,0,2:T(8,128)S(1)}, u32[]{:S(2)}, u32[]{:S(2)}) collective-permute-start(f32[67,67,3]{1,0,2:T(8,128)S(1)} %copy.17), channel_id=1, source_target_pairs={{0,16},{16,0},{1,17},{17,1},{2,18},{18,2},{3,19},{19,3},{4,20},{20... | collective-permute-start | bytes 161612 | tf_op jit(solution)/shard_map/ppermute | solution.py:24
  42.0 2.4 slice.78
  44.4 3.0 collective-permute-done
  47.4 2.3 copy.18
  49.8 2.7 slice_add_fusion
  52.5 0.1 pad_maximum_fusion.7
  52.6 1.6 collective-permute-start.1
  54.2 4.1 %collective-permute-done.1 = f32[3,67,128]{2,1,0:T(8,128)S(1)} collective-permute-done((f32[3,67,128]{2,1,0:T(8,128)S(1)}, f32[3,67,128]{2,1,0:T(8,128)S(1)}, u32[]{:S(2)}, u32[]{:S(2)}) %collective-permute-start.1) | collective-permute-done | bytes 102944 | tf_op jit(solution)/shard_map/ppermute | solution.py:24
  58.3 0.1 maximum_add_fusion
  58.4 0.7 fusion.10
  59.1 0.1 collective-permute-start.2
  59.2 0.3 slice.81
  59.5 4.1 %collective-permute-done.2 = f32[64,3,128]{2,1,0:T(4,128)S(1)} collective-permute-done((f32[64,3,128]{2,1,0:T(4,128)S(1)}, f32[64,3,128]{2,1,0:T(4,128)S(1)}, u32[]{:S(2)}, u32[]{:S(2)}) %collective-permute-start.2) | collective-permute-done | bytes 98336 | tf_op jit(solution)/shard_map/ppermute | solution.py:24
  63.6 0.5 pad_maximum_fusion.3
  64.1 1.2 copy.19
  65.3 28.3 %all_to_all.30 = f32[4,16,64,128]{3,1,2,0:T(8,128)S(1)} all-to-all(f32[4,16,64,128]{3,1,2,0:T(8,128)S(1)} %copy.19), channel_id=1, replica_groups=mesh['gz'=2,'gy'=4,'gx'=4] {'gy'}, dimensions={0} | all-to-all | bytes 4194304 | tf_op jit(solution)/shard_map/all_to_all | solution.py:186
  93.6 1.6 fusion.20
  95.2 30.3 %all_to_all.31 = f32[16,16,2048]{2,1,0:T(8,128)S(1)} all-to-all(f32[16,16,2048]{2,1,0:T(8,128)S(1)} %bitcast.113), channel_id=1, replica_groups=mesh['gz'=2,'gy'=4,'gx'=4] {'gx','gy'}, dimensions={0} | all-to-all | bytes 4194304 | tf_op jit(solution)/shard_map/all_to_all | solution.py:186
  125.5 3.3 fusion.17
  128.8 4.1 %all-to-all-start.2 = ((f32[2,256,1024]{2,1,0:T(8,128)}), f32[2,256,1024]{2,1,0:T(8,128)S(1)}, u32[]{:S(2)}, u32[]{:S(2)}) async-start(f32[2,256,1024]{2,1,0:T(8,128)} %bitcast.110), calls=%async_computation.2 | async-start | bytes 4194304 | tf_op jit(solution)/shard_map/all_to_all | solution.py:186
  133.1 0.1 add_bitcast_fusion
  133.2 0.1 multiply_bitcast_fusion
  133.3 0.5 fusion.36
  133.8 46.6 %all-to-all-done.2 = f32[2,256,1024]{2,1,0:T(8,128)S(1)} async-done(((f32[2,256,1024]{2,1,0:T(8,128)}), f32[2,256,1024]{2,1,0:T(8,128)S(1)}, u32[]{:S(2)}, u32[]{:S(2)}) %all-to-all-start.2) | async-done | bytes 2097184 | tf_op jit(solution)/shard_map/all_to_all | solution.py:186
  180.4 1.8 copy.27
  182.2 2.0 copy.20
  184.3 3.4 bitcast_multiply_fusion
  187.7 1.9 fusion.58
  189.6 48.8 %all_to_all.32 = f32[2,256,1024]{2,1,0:T(8,128)S(1)} all-to-all(f32[2,256,1024]{2,1,0:T(8,128)S(1)} %bitcast.115), channel_id=1, replica_groups=mesh['gz'=2,'gy'=4,'gx'=4] {'gz'}, dimensions={0} | all-to-all | bytes 4194304 | tf_op jit(solution)/shard_map/all_to_all | solution.py:186
  238.5 1.8 copy.29
  240.3 2.1 copy.21
  242.4 2.0 fusion.11
  244.4 30.6 %all_to_all.33 = f32[16,32,1024]{2,1,0:T(8,128)S(1)} all-to-all(f32[16,32,1024]{2,1,0:T(8,128)S(1)} %bitcast.117), channel_id=1, replica_groups=mesh['gz'=2,'gy'=4,'gx'=4] {'gx','gy'}, dimensions={0} | all-to-all | bytes 4194304 | tf_op jit(solution)/shard_map/all_to_all | solution.py:186
  275.1 0.5 copy.31
  275.5 0.5 copy-done.5
  276.0 1.2 fusion.59
  277.2 28.1 %all_to_all.34 = f32[4,64,2048]{2,1,0:T(8,128)S(1)} all-to-all(f32[4,64,2048]{2,1,0:T(8,128)S(1)} %bitcast.119), channel_id=1, replica_groups=mesh['gz'=2,'gy'=4,'gx'=4] {'gy'}, dimensions={0} | all-to-all | bytes 4194304 | tf_op jit(solution)/shard_map/all_to_all | solution.py:186
  305.3 0.4 copy.32
  305.7 0.1 bitcast_bitcast_fusion
  305.9 0.6 copy.22
  306.5 0.6 collective-permute-start.3
  307.1 4.1 %collective-permute-done.3 = f32[3,64,128]{2,1,0:T(8,128)S(1)} collective-permute-done((f32[3,64,128]{2,1,0:T(8,128)S(1)}, f32[3,64,128]{2,1,0:T(8,128)S(1)}, u32[]{:S(2)}, u32[]{:S(2)}) %collective-permute-start.3) | collective-permute-done | bytes 98336 | tf_op jit(solution)/shard_map/ppermute | solution.py:24
  311.2 0.1 collective-permute-start.4
  311.3 2.6 collective-permute-done.4
  313.9 1.6 pad_maximum_fusion.1
  315.5 3.3 copy.23
  318.9 0.3 collective-permute-start.5
  319.2 3.4 pad_maximum_fusion.4
  322.6 5.5 %collective-permute-done.5 = f32[67,67,3]{1,0,2:T(8,128)} collective-permute-done((f32[67,67,3]{1,0,2:T(8,128)}, f32[67,67,3]{1,0,2:T(8,128)}, u32[]{:S(2)}, u32[]{:S(2)}) %collective-permute-start.5) | collective-permute-done | bytes 53900 | tf_op jit(solution)/shard_map/ppermute | solution.py:24
  328.0 3.2 copy.24
  331.2 2.6 fusion.9
  333.8 8.2 %fusion.8.pot_ref = bf16[68,80,393]{2,1,0:T(8,128)(2,1)} fusion(bf16[67,67,131]{2,1,0:T(8,128)(2,1)S(1)} %get-tuple-element.8, bf16[67,67,131]{2,1,0:T(8,128)(2,1)S(1)} %get-tuple-element.7), kind=kLoop, calls=%fused_computation.12 | loop fusion | flops 32068800 | bytes 6628076 | tf_op jit(solution)/shard_map/concatenate | solution.py:148
  342.0 53.4 %shard_map.101 = f32[3,2048]{1,0:T(4,128)} custom-call(bf16[68,80,393]{2,1,0:T(8,128)(2,1)} %fusion.8.pot_ref, bf16[393,2048]{1,0:T(8,128)(2,1)} %get-tuple-element.54.z_ref, bf16[393,2048]{1,0:T(8,128)(2,1)} %get-tuple-element.55.gz_ref, f32[80,2048]{1,0:T(8,128)} %get-tuple-element.47.y_ref, f32[80,2048]{1,0:T(8,128)} %get-tuple-element.46.gy_ref, ...), custom_call_target="tpu_custom_call" | custom-call | tf_op jit(solution)/shard_map/pallas_call | solution.py:160
  395.4 1.4 broadcast_multiply_fusion
  (20 shorter events, 0.3 us)
Async XLA Ops:
  37.9 9.5 %collective-permute-start = (f32[67,67,3]{1,0,2:T(8,128)S(1)}, f32[67,67,3]{1,0,2:T(8,128)S(1)}, u32[]{:S(2)}, u32[]{:S(2)}) collective-permute-start(f32[67,67,3]{1,0,2:T(8,128)S(1)} %copy.17), channel_id=1, source_target_pairs={{0,16},{16,0},{1,17},{17,1},{2,18},{18,2},{3,19},{19,3},{4,20},{20... | collective-permute-start | bytes 161612 | tf_op jit(solution)/shard_map/ppermute | solution.py:24
  52.6 5.7 %collective-permute-start.1 = (f32[3,67,128]{2,1,0:T(8,128)S(1)}, f32[3,67,128]{2,1,0:T(8,128)S(1)}, u32[]{:S(2)}, u32[]{:S(2)}) collective-permute-start(f32[3,67,128]{2,1,0:T(8,128)S(1)} %pad_maximum_fusion.7), channel_id=1, source_target_pairs={{0,1},{1,2},{2,3},{3,0},{4,5},{5,6},{6,7},{7,4},{8,9},{9,10},{10,1... | collective-permute-start | bytes 308744 | tf_op jit(solution)/shard_map/ppermute | solution.py:24
  59.1 4.4 %collective-permute-start.2 = (f32[64,3,128]{2,1,0:T(4,128)S(1)}, f32[64,3,128]{2,1,0:T(4,128)S(1)}, u32[]{:S(2)}, u32[]{:S(2)}) collective-permute-start(f32[64,3,128]{2,1,0:T(4,128)S(1)} %slice.80), channel_id=1, source_target_pairs={{0,4},{4,8},{8,12},{12,0},{1,5},{5,9},{9,13},{13,1},{2,6},{6,10},{... | collective-permute-start | bytes 294920 | tf_op jit(solution)/shard_map/ppermute | solution.py:24
  65.3 28.3 %copy-start.6 = (f32[256,256]{1,0:T(8,128)S(1)}, f32[256,256]{1,0:T(8,128)}, u32[]{:S(2)}) copy-start(f32[256,256]{1,0:T(8,128)} %constant.35.clone) | copy-start | bytes 786436
  95.2 30.3 %copy-start.4 = (f32[512,512]{1,0:T(8,128)S(1)}, f32[512,512]{1,0:T(8,128)}, u32[]{:S(2)}) copy-start(f32[512,512]{1,0:T(8,128)} %constant.36.clone) | copy-start | bytes 3145732
  128.8 51.6 %all-to-all-start.2 = ((f32[2,256,1024]{2,1,0:T(8,128)}), f32[2,256,1024]{2,1,0:T(8,128)S(1)}, u32[]{:S(2)}, u32[]{:S(2)}) async-start(f32[2,256,1024]{2,1,0:T(8,128)} %bitcast.110), calls=%async_computation.2 | async-start | bytes 4194304 | tf_op jit(solution)/shard_map/all_to_all | solution.py:186
  184.3 3.4 copy-start.3
  240.3 2.1 copy-start.2
  275.1 1.0 copy-start.5
  306.5 4.7 %collective-permute-start.3 = (f32[3,64,128]{2,1,0:T(8,128)S(1)}, f32[3,64,128]{2,1,0:T(8,128)S(1)}, u32[]{:S(2)}, u32[]{:S(2)}) collective-permute-start(f32[3,64,128]{2,1,0:T(8,128)S(1)} %slice.82), channel_id=1, source_target_pairs={{0,3},{1,0},{2,1},{3,2},{4,7},{5,4},{6,5},{7,6},{8,11},{9,8},{10,9... | collective-permute-start | bytes 294920 | tf_op jit(solution)/shard_map/ppermute | solution.py:24
  311.2 2.6 collective-permute-start.4
  315.5 3.6 copy-start
  315.5 3.6 copy-start.1
  318.9 9.2 %collective-permute-start.5 = (f32[67,67,3]{1,0,2:T(8,128)}, f32[67,67,3]{1,0,2:T(8,128)}, u32[]{:S(2)}, u32[]{:S(2)}) collective-permute-start(f32[67,67,3]{1,0,2:T(8,128)} %copy.23), channel_id=1, source_target_pairs={{0,16},{16,0},{1,17},{17,1},{2,18},{18,2},{3,19},{19,3},{4,20},{20... | collective-permute-start | bytes 161612 | tf_op jit(solution)/shard_map/ppermute | solution.py:24
